TPU v7x, 256 devices: a 8x8x2 block of a 8x8x16 slice. The times are simulated.
256 devices in a mesh: groups: 2 (over z), patch: 128 (over x, y, core).
Axes of the slice: x: 8, y: 8, z: 2, core: 2. Of those that a mesh axis runs over, the one named last changes fastest.
The devices are a block of a 8x8x16 slice.
Arguments:
- queries: bfloat16 [8192, 1536], P(('groups', 'patch')), parts along dimension 0, may hold values from -8 to 8
- fresh_keys: bfloat16 [8192, 1536], P(('groups', 'patch')), parts along dimension 0, may hold values from -8 to 8
- fresh_values: bfloat16 [8192, 1536], P(('groups', 'patch')), parts along dimension 0, may hold values from -128 to 128
- stale_keys: bfloat16 [8192, 1536], P(('groups', 'patch')), parts along dimension 0, may hold values from -8 to 8
- stale_values: bfloat16 [8192, 1536], P(('groups', 'patch')), parts along dimension 0, may hold values from -128 to 128
- text_keys: bfloat16 [452, 1536], P('groups'), parts along dimension 0, may hold values from -8 to 8
- text_values: bfloat16 [452, 1536], P('groups'), parts along dimension 0, may hold values from -128 to 128
- out_weight: bfloat16 [1536, 3072], P(None, 'patch'), may hold values from -0.15625 to 0.15625
- gate_table: float32 [50, 3072], replicated, may hold values from 0.1 to 1.9
- timestep: int32 [2], P('groups'), parts along dimension 0, may hold values from 0 to 49
Outputs:
- branch: bfloat16 [8192, 3072], P(('groups', 'patch')), parts along dimension 0
There are 2 independent parts, one for each index of `groups`. A program takes and returns all parts, laid end to end along the dimension named above; an argument that names none is the same for every part. Nothing has to cross between parts.
All inputs are finite; a program needn't handle non-finite values.
Results may differ from a plain program's by a relative error of at most 0.0095.
Values may be sent and summed in bfloat16 or wider, within the bound.
A program may use at most 128 MiB of HBM per device.

v0:
```python
import jax
import jax.numpy as jnp
from jax import lax
from jax.sharding import PartitionSpec as P

HEAD_DIM = 64
HEADS = 24


def sent_together(arrays, axis, dim, along):
    ends, at = ([], 0)
    for a in arrays[:-1]:
        at += a.shape[along]
        ends.append(at)
    both = jnp.concatenate(arrays, axis=along)
    return tuple(jnp.split(lax.all_gather(both, axis, axis=dim, tiled=True), ends, axis=along))


def body(
    queries,
    fresh_keys,
    fresh_values,
    stale_keys,
    stale_values,
    text_keys,
    text_values,
    out_weight,
    gate_table,
    timestep,
):
    row_count = queries.shape[0]
    head_count = HEADS
    head_width = HEAD_DIM
    scaling = head_width ** (-0.5)
    query = queries.reshape(row_count, head_count, head_width)

    def scores_for(key_block):
        shaped = key_block.reshape(key_block.shape[0], head_count, head_width)
        return (
            jnp.einsum("thd,shd->ths", query, shaped, preferred_element_type=jnp.float32) * scaling
        )

    def weigh(expo, value_block):
        shaped = value_block.reshape(value_block.shape[0], head_count, head_width)
        return jnp.einsum(
            "ths,shd->thd", expo.astype(jnp.bfloat16), shaped, preferred_element_type=jnp.float32
        )

    near_keys = jnp.concatenate([text_keys, fresh_keys], 0)
    near_values = jnp.concatenate([text_values, fresh_values], 0)
    near_scores = scores_for(near_keys)
    running_max = jnp.max(near_scores, -1)
    near_expo = jnp.exp(near_scores - running_max[..., None])
    running_sum = jnp.sum(near_expo, -1)
    weighted = weigh(near_expo, near_values)
    own_first = lax.axis_index("patch") * row_count
    key_part, value_part = sent_together((stale_keys, stale_values), "patch", 0, 1)
    positions = jnp.arange(key_part.shape[0], dtype=jnp.int32)
    remote_mask = (positions < own_first) | (positions >= own_first + row_count)
    scores = jnp.where(remote_mask[None, None, :], scores_for(key_part), -1e30)
    new_max = jnp.maximum(running_max, jnp.max(scores, -1))
    shrink = jnp.exp(running_max - new_max)
    expo = jnp.exp(scores - new_max[..., None])
    new_sum = running_sum * shrink + jnp.sum(expo, -1)
    new_weighted = weighted * shrink[..., None] + weigh(expo, value_part)
    attended = (
        (new_weighted / new_sum[..., None])
        .reshape(row_count, head_count * head_width)
        .astype(jnp.bfloat16)
    )
    projected = jnp.dot(
        attended,
        lax.all_gather(out_weight, "patch", axis=1, tiled=True),
        preferred_element_type=jnp.float32,
    )
    selector = (jnp.arange(gate_table.shape[0], dtype=jnp.int32) == timestep[0]).astype(jnp.float32)
    gating = jnp.dot(selector, gate_table, precision=lax.Precision.HIGHEST)
    return (projected * gating[None, :]).astype(jnp.bfloat16)


def solution(mesh):
    in_specs = (
        P(("groups", "patch"), None),
        P(("groups", "patch"), None),
        P(("groups", "patch"), None),
        P(("groups", "patch"), None),
        P(("groups", "patch"), None),
        P("groups", None),
        P("groups", None),
        P(None, "patch"),
        P(),
        P("groups"),
    )
    out_specs = P(("groups", "patch"), None)
    return jax.shard_map(body, mesh=mesh, in_specs=in_specs, out_specs=out_specs, check_vma=False)
```

profile of v0, /device:TPU:514, one launch (start us, length us, event | category | flops | bytes accessed | tf_op | source)
XLA Modules:
  0.0 245.3 jit_solution(3291035466819410238)
XLA Ops:
  6.5 0.0 copy-start
  6.6 0.0 all-gather.3.cloned.1.call-start
  6.6 1.7 pad_maximum_fusion.2
  8.3 0.1 all-gather.3.cloned.1.call-update
  8.3 0.1 all-gather.5.cloned.1.call-start
  8.4 0.7 all-gather.5.cloned.1.call-update
  9.1 1.1 reshape.49
  10.2 1.2 pad_maximum_fusion.1
  11.4 0.7 copy.18
  12.2 1.2 pad_maximum_fusion
  13.4 1.4 copy.17
  15.5 0.4 fusion.34
  15.9 0.4 fusion.18
  16.3 0.0 copy-done
  16.3 0.3 fusion.26
  16.6 128.5 %all-gather.3.cloned.1.call-done = bf16[4096,3072]{1,0:T(8,128)(2,1)} async-done(((bf16[32,3072]{1,0:T(8,128)(2,1)}), bf16[4096,3072]{1,0:T(8,128)(2,1)}) %all-gather.3.cloned.1.call-update) | async-done | bytes 25165840 | tf_op jit(solution)/shard_map/all_gather | solution.py:16
  145.1 17.1 %fusion.33 = (bf16[4096,1536]{1,0:T(8,128)(2,1)}, bf16[4096,1536]{1,0:T(8,128)(2,1)}) fusion(bf16[4096,3072]{1,0:T(8,128)(2,1)} %all-gather.3.cloned.1.call-done), kind=kLoop, calls=%fused_computation.43 | loop fusion | bytes 50331648 | tf_op jit(solution)/shard_map/split | solution.py:16
  162.2 16.5 %copy.22 = bf16[4096,1536]{0,1:T(8,128)(2,1)} copy(bf16[4096,1536]{1,0:T(8,128)(2,1)} %get-tuple-element.8) | data formatting | bytes 25165824 | tf_op jit(solution)/shard_map/split | solution.py:16
  178.7 16.8 %copy.20 = bf16[4096,1536]{0,1:T(8,128)(2,1)} copy(bf16[4096,1536]{1,0:T(8,128)(2,1)} %get-tuple-element.7) | data formatting | bytes 25165824 | tf_op jit(solution)/shard_map/split | solution.py:16
  195.5 6.4 %bitcast_reduce_fusion = (f32[32,24]{0,1:T(8,128)S(1)}, f32[24,4096,32]{1,2,0:T(8,128)S(1)}) fusion(pred[4096]{0:T(1024)(128)(4,1)S(1)} %fusion.25, bf16[4096,24,64]{0,2,1:T(8,128)(2,1)} %bitcast.43, bf16[32,24,64]{2,1,0:T(8,128)(2,1)S(1)} %reshape.49), kind=kOutput, calls=%fused_computation.1 | convolution fusion | flops 412089600 | bytes 25271296 | tf_op jit(solution)/shard_map/thd,shd->ths/dot_general | solution.py:40
  201.9 0.0 copy-start.2
  201.9 4.6 %copy-done.2 = f32[24,4096,32]{1,2,0:T(8,128)} copy-done((f32[24,4096,32]{1,2,0:T(8,128)}, f32[24,4096,32]{1,2,0:T(8,128)S(1)}, u32[]{:S(2)}) %copy-start.2) | copy-done | bytes 12582936
  206.5 3.0 %fusion.1 = f32[32,24]{0,1:T(8,128)S(1)} fusion(f32[24,4096,32]{1,2,0:T(8,128)S(1)} %get-tuple-element.12, f32[32,24]{0,1:T(8,128)S(1)} %max.13, pred[4096]{0:T(1024)(128)(4,1)S(1)} %fusion.25), kind=kLoop, calls=%fused_computation.4 | loop fusion | flops 12582144 | bytes 12593152 | tf_op jit(solution)/shard_map/reduce_sum | solution.py:64
  209.5 0.0 copy-start.3
  209.5 0.0 copy-start.1
  209.5 10.8 %fusion.14 = f32[32,24,64]{2,0,1:T(8,128)S(1)} fusion(bf16[4096,24,64]{0,2,1:T(8,128)(2,1)} %bitcast.44, f32[24,4096,32]{1,2,0:T(8,128)} %copy-done.2, f32[32,24]{0,1:T(8,128)S(1)} %max.13, pred[4096]{0:T(1024)(128)(4,1)S(1)} %fusion.25), kind=kOutput, calls=%fused_computation.19 | convolution fusion | flops 415236096 | bytes 25369600 | tf_op jit(solution)/shard_map/ths,shd->thd/dot_general | solution.py:45
  220.3 0.0 copy-done.3
  220.4 0.6 fusion.17
  221.0 0.1 copy.23
  221.1 0.2 convert_element_type.19
  221.3 10.0 %all-gather.5.cloned.1.call-done = bf16[1536,3072]{0,1:T(8,128)(2,1)} async-done(((bf16[1536,24]{0,1:T(8,128)(2,1)}), bf16[1536,3072]{0,1:T(8,128)(2,1)}) %all-gather.5.cloned.1.call-update) | async-done | bytes 9437200 | tf_op jit(solution)/shard_map/all_gather | solution.py:73
  231.2 7.2 %fusion.9 = bf16[32,3072]{1,0:T(8,128)(2,1)} fusion(bf16[32,1536]{1,0:T(8,128)(2,1)S(1)} %convert_element_type.19, bf16[1536,3072]{0,1:T(8,128)(2,1)} %all-gather.5.cloned.1.call-done, f32[3072]{0:T(1024)S(1)} %bitcast.47), kind=kOutput, calls=%fused_computation.12 | convolution fusion | flops 302186496 | bytes 9744384 | tf_op jit(solution)/shard_map/dot_general | solution.py:71
  238.4 0.0 copy-done.1
  (3 shorter events, 0.0 us)
Async XLA Ops:
  6.5 9.7 %copy-start = (f32[50,3072]{1,0:T(8,128)S(1)}, f32[50,3072]{1,0:T(8,128)}, u32[]{:S(2)}) copy-start(f32[50,3072]{1,0:T(8,128)} %param.18) | copy-start | bytes 1843204
  6.6 138.5 %all-gather.3.cloned.1.call-start = ((), (), s32[]{:S(2)}) async-start(), calls=%async_computation | async-start | bytes 25362432 | tf_op jit(solution)/shard_map/all_gather | solution.py:16
  8.3 222.9 %all-gather.5.cloned.1.call-start = ((), (), s32[]{:S(2)}) async-start(), calls=%async_computation.1 | async-start | bytes 9510912 | tf_op jit(solution)/shard_map/all_gather | solution.py:73
  201.9 4.6 %copy-start.2 = (f32[24,4096,32]{1,2,0:T(8,128)}, f32[24,4096,32]{1,2,0:T(8,128)S(1)}, u32[]{:S(2)}) copy-start(f32[24,4096,32]{1,2,0:T(8,128)S(1)} %get-tuple-element.12) | copy-start | bytes 37748740
  209.5 10.9 %copy-start.3 = (bf16[258,1536]{0,1:T(8,128)(2,1)S(1)}, bf16[258,1536]{0,1:T(8,128)(2,1)}, u32[]{:S(2)}) copy-start(bf16[258,1536]{0,1:T(8,128)(2,1)} %copy.17) | copy-start | bytes 2377732
  209.5 28.9 %copy-start.1 = (f32[50,3072]{1,0:T(8,128)S(1)}, f32[50,3072]{1,0:T(8,128)}, u32[]{:S(2)}) copy-start(f32[50,3072]{1,0:T(8,128)} %param.18) | copy-start | bytes 1843204
Sparse Core Ops, SparseCore 0:
  9.9 135.1 all-gather.2
  147.7 83.4 all-gather.4
where the time goes:
time: 248 us; the launch traced here: 245 us
  waiting for transfers between devices  139 us (56%)
  local copies, waits for them, and re-layouts  58.4 us (24%)
  matrix products  25.8 us (10%)
  between operations  14.2 us (6%)
  other arithmetic  7.58 us (3%)
    all_gather x1, waiting for transfers between devices, sent_together(): lax.all_gather(both, axis, axis=dim, tiled=True)  128 us
    split x3, local copies, waits for them, and re-layouts, sent_together(): jnp.split(lax.all_gather(both, axis, axis=dim, tiled=True), ends, axis=al...  50.4 us
    dot_general x2, matrix products, weigh(): jnp.einsum('ths,shd->thd', expo.astype(jnp.bfloat16), shaped, preferred_e...  11.5 us
    all_gather x1, waiting for transfers between devices, body(): lax.all_gather(out_weight, 'patch', axis=1, tiled=True)  9.96 us
    dot_general x1, matrix products, body(): jnp.dot(attended, lax.all_gather(out_weight, 'patch', axis=1, tiled=True)...  7.19 us
    dot_general x2, matrix products, scores_for(): jnp.einsum('thd,shd->ths', query, shaped, preferred_element_type=jnp.floa...  6.84 us
  transfers between devices with their start and end apart: 2, of which 2 were waited for; matrix products, arithmetic and copies ran while one was open for 32% of the time, Pallas kernels for 0%

commit v1 on v0

v1 whole, which is shorter than its diff:
```python
import functools
import math

import jax
import jax.numpy as jnp
from jax import lax
from jax.experimental import pallas as pl
from jax.experimental.pallas import tpu as pltpu
from jax.sharding import PartitionSpec as P

HEAD_DIM = 64
HEADS = 24
LANES = 128
SUBS = 4
O_SUBS = 2
MESH = pl.DeviceIdType.MESH
F32 = jnp.float32
BF16 = jnp.bfloat16


def swap_halves(tile):
    return pltpu.roll(tile.astype(F32), HEAD_DIM, 1).astype(tile.dtype)


def kernel(
    side,
    q_hbm,
    fk_hbm,
    fv_hbm,
    sk_hbm,
    sv_hbm,
    tk_hbm,
    tv_hbm,
    w_hbm,
    gate_hbm,
    step_ref,
    o_ref,
    q_v,
    fk_v,
    fv_v,
    sk_v,
    sv_v,
    tk_v,
    tv_v,
    w_v,
    gate_v,
    pack_kv,
    pack_q,
    pack_f,
    kv,
    fresh,
    q_in,
    qb,
    text,
    m_s,
    l_s,
    acc,
    og,
    wg,
    wcat,
    att,
    out_send,
    out_in,
    in_sem,
    xk_s,
    xk_r,
    xq_s,
    xq_r,
    xf_s,
    xf_r,
    yk_s,
    yk_r,
    ck_s,
    ck_r,
    yw_s,
    yw_r,
    cw_s,
    cw_r,
    xo_s,
    xo_r,
    oo_s,
    oo_r,
):
    rows = q_v.shape[0]
    half_rows = rows // 2
    group = HEADS // side
    q_half = side * half_rows
    q_all = 2 * q_half
    chunk = side * rows
    sub = chunk // SUBS
    reach = side // 2
    n_text = tk_v.shape[0]
    block = w_v.shape[1] * 2 * side
    factor = HEAD_DIM ** (-0.5) * math.log2(math.e)

    me = lax.axis_index("patch")
    core = lax.rem(me, 2)
    y = lax.rem(lax.div(me, 2), side)
    x = lax.div(me, 2 * side)

    def wrap(value):
        return lax.rem(value + side, side)

    def at_x(offset):
        return {"patch": (wrap(x + offset) * side + y) * 2 + core}

    def at_y(offset):
        return {"patch": (x * side + wrap(y + offset)) * 2 + core}

    partner = {"patch": (x * side + y) * 2 + 1 - core}

    offsets = [0]
    for k in range(1, reach):
        offsets += [k, -k]
    offsets.append(reach)

    def slot_of(offset):
        return offsets.index(offset) if offset in offsets else offsets.index(offset + side)

    def remote(src, dst, send_sem, recv_sem, device):
        return pltpu.make_async_remote_copy(
            src_ref=src,
            dst_ref=dst,
            send_sem=send_sem,
            recv_sem=recv_sem,
            device_id=device,
            device_id_type=MESH,
        )

    cols_x = pl.ds(pl.multiple_of(x * block, LANES), block)
    loads = [
        pltpu.make_async_copy(src, dst, in_sem.at[i])
        for i, (src, dst) in enumerate(
            [
                (sk_hbm, sk_v),
                (sv_hbm, sv_v),
                (q_hbm, q_v),
                (fk_hbm, fk_v),
                (fv_hbm, fv_v),
                (w_hbm, w_v),
                (tk_hbm, tk_v),
                (tv_hbm, tv_v),
                (gate_hbm.at[:, cols_x], gate_v),
            ]
        )
    ]
    for load in loads:
        load.start()

    barrier = pltpu.get_barrier_semaphore()
    peers = [at_x(o) for o in offsets[1:]] + [at_y(1), at_y(-1), partner]
    for peer in peers:
        pl.semaphore_signal(barrier, inc=1, device_id=peer, device_id_type=MESH)

    def low(shape):
        return lax.broadcasted_iota(jnp.int32, shape, 1) < HEAD_DIM

    def pack_pairs(k_ref, v_ref, out):
        is_low = low((rows, LANES))
        for pair in range(HEADS // 2):
            cols = slice(pair * LANES, (pair + 1) * LANES)
            k, v = k_ref[:, cols], v_ref[:, cols]
            even, odd = 2 * pair, 2 * pair + 1
            out[even // group, even % group] = jnp.where(is_low, k, swap_halves(v))
            out[odd // group, odd % group] = jnp.where(is_low, swap_halves(k), v)

    own = y * 2 + core

    def slot_rows(slot):
        return pl.ds(slot * rows, rows)

    loads[0].wait()
    loads[1].wait()
    pack_pairs(sk_v, sv_v, pack_kv)
    pl.semaphore_wait(barrier, len(peers))

    def x_kv(offset):
        back = slot_of(-offset)
        return remote(
            pack_kv.at[wrap(x + offset)],
            kv.at[own, :, slot_rows(back), :],
            xk_s.at[slot_of(offset)],
            xk_r.at[back],
            at_x(offset),
        )

    def x_kv_wait(slot):
        remote(
            pack_kv.at[x],
            kv.at[own, :, slot_rows(slot), :],
            xk_s.at[slot],
            xk_r.at[slot],
            at_x(-offsets[slot]),
        ).wait_recv()

    for o in offsets[1:]:
        x_kv(o).start()
    kv[own, :, 0:rows, :] = pack_kv[x]

    loads[2].wait()
    is_low = low((half_rows, LANES))
    for pair in range(HEADS // 2):
        cols = slice(pair * LANES, (pair + 1) * LANES)
        top, bottom = q_v[0:half_rows, cols], q_v[half_rows:rows, cols]
        even, odd = 2 * pair, 2 * pair + 1
        pack_q[even // group, even % group] = jnp.where(is_low, top, swap_halves(bottom))
        pack_q[odd // group, odd % group] = jnp.where(is_low, swap_halves(top), bottom)

    def x_q(offset):
        return remote(
            pack_q.at[wrap(x + offset)],
            q_in.at[x],
            xq_s.at[slot_of(offset)],
            xq_r.at[slot_of(-offset)],
            at_x(offset),
        )

    loads[3].wait()
    loads[4].wait()
    pack_pairs(fk_v, fv_v, pack_f)

    def x_f(offset):
        return remote(
            pack_f.at[wrap(x + offset)],
            fresh.at[:, pl.ds(pl.multiple_of(x * rows, rows), rows), :],
            xf_s.at[slot_of(offset)],
            xf_r.at[slot_of(-offset)],
            at_x(offset),
        )

    for o in offsets[1:]:
        x_q(o).start()
    for o in offsets[1:]:
        x_f(o).start()
    q_in[x] = pack_q[x]
    fresh[:, pl.ds(pl.multiple_of(x * rows, rows), rows), :] = pack_f[x]

    loads[5].wait()
    w_cols = w_v.shape[1]
    unit = (
        lax.broadcasted_iota(jnp.int32, (w_cols, w_cols), 0)
        == lax.broadcasted_iota(jnp.int32, (w_cols, w_cols), 1)
    ).astype(BF16)
    wg[own] = lax.dot_general(
        unit, w_v[...], (((1,), (1,)), ((), ())), preferred_element_type=F32
    ).astype(BF16)

    def origin(direction, hops):
        return wrap(y - hops if direction == 0 else y + hops) * 2 + core

    def kv_piece(index, u):
        return kv.at[index, :, pl.ds(u * sub, sub), :]

    def kv_hop(direction, hops, u):
        piece = kv_piece(origin(direction, hops), u)
        return remote(
            piece,
            piece,
            yk_s.at[direction, hops, u],
            yk_r.at[direction, hops, u],
            at_y(1 if direction == 0 else -1),
        )

    def kv_arrival(direction, hops, u):
        piece = kv_piece(origin(direction, hops), u)
        remote(
            piece,
            piece,
            yk_s.at[direction, hops - 1, u],
            yk_r.at[direction, hops - 1, u],
            at_y(-1 if direction == 0 else 1),
        ).wait_recv()

    def rel(direction, hops):
        return hops if direction == 0 or hops == reach else reach + hops

    def kv_share(direction, hops, u):
        piece = kv_piece(origin(direction, hops), u)
        index = rel(direction, hops)
        return remote(piece, piece, ck_s.at[index, u], ck_r.at[index, u], partner)

    def other(direction, hops):
        return wrap(y - hops if direction == 0 else y + hops) * 2 + 1 - core

    def kv_shared(direction, hops, u):
        piece = kv_piece(other(direction, hops), u)
        index = rel(direction, hops)
        remote(piece, piece, ck_s.at[index, u], ck_r.at[index, u], partner).wait_recv()

    def carries(direction, u):
        return (u < SUBS // 2) == (direction == 0)

    def w_hop(direction, hops):
        piece = wg.at[origin(direction, hops)]
        return remote(
            piece,
            piece,
            yw_s.at[direction, hops],
            yw_r.at[direction, hops],
            at_y(1 if direction == 0 else -1),
        )

    def w_arrival(direction, hops):
        piece = wg.at[origin(direction, hops)]
        remote(
            piece,
            piece,
            yw_s.at[direction, hops - 1],
            yw_r.at[direction, hops - 1],
            at_y(-1 if direction == 0 else 1),
        ).wait_recv()

    def w_share(direction, hops):
        piece = wg.at[origin(direction, hops)]
        index = rel(direction, hops)
        return remote(piece, piece, cw_s.at[index], cw_r.at[index], partner)

    def w_shared(direction, hops):
        piece = wg.at[other(direction, hops)]
        index = rel(direction, hops)
        remote(piece, piece, cw_s.at[index], cw_r.at[index], partner).wait_recv()

    sends = []

    def go(copy):
        copy.start()
        sends.append(copy)

    go(w_hop(0, 0))
    go(w_hop(1, 0))
    go(w_share(0, 0))

    per_sub = side // SUBS
    for u in range(SUBS):
        for slot in range(u * per_sub, (u + 1) * per_sub):
            if slot:
                x_kv_wait(slot)
        go(kv_hop(0, 0, u))
        go(kv_hop(1, 0, u))
        go(kv_share(0, 0, u))

    loads[6].wait()
    loads[7].wait()
    text[:, text.shape[1] - 32 :, :] = jnp.zeros((group, 32, LANES), BF16)
    is_low_text = low((n_text, LANES))
    for i in range(group):
        head = x * group + i
        odd = jnp.broadcast_to(lax.rem(head, 2), (n_text, LANES)) == 1
        cols = pl.ds(pl.multiple_of(lax.div(head, 2) * LANES, LANES), LANES)
        k, v = tk_v[:, cols], tv_v[:, cols]
        k = jnp.where(odd, swap_halves(k), k)
        v = jnp.where(odd, v, swap_halves(v))
        text[i, 0:n_text, :] = jnp.where(is_low_text, k, v)

    def attend(pieces, keep=None, first=False):
        def one_head(i, carry):
            keys = jnp.concatenate([piece(i) for piece in pieces], axis=0)
            scores = lax.dot_general(
                qb[i], keys, (((1,), (1,)), ((), ())), preferred_element_type=F32
            )
            if keep is not None:
                scores = jnp.where(keep(scores.shape), scores, -jnp.inf)
            width = scores.shape[1] // LANES
            highest = jnp.max(scores, axis=1, keepdims=True)
            if first:
                new_m = jnp.broadcast_to(highest, (q_all, LANES))
            else:
                old_m = m_s[i]
                new_m = jnp.maximum(old_m, highest)
            expo = jnp.exp2((scores - jnp.concatenate([new_m] * width, axis=1)) * factor)
            part = expo[:, 0:LANES]
            for k in range(1, width):
                part = part + expo[:, k * LANES : (k + 1) * LANES]
            weighted = jnp.dot(expo.astype(BF16), keys, preferred_element_type=F32)
            if first:
                l_s[i] = part
                acc[i] = weighted
            else:
                shrink = jnp.exp2((old_m - new_m) * factor)
                l_s[i] = l_s[i] * shrink + part
                acc[i] = acc[i] * shrink + weighted
            m_s[i] = new_m
            return carry

        lax.fori_loop(0, group, one_head, 0)

    def start_queries():
        for slot in range(1, side):
            remote(
                pack_q.at[x],
                q_in.at[wrap(x + offsets[slot])],
                xq_s.at[slot],
                xq_r.at[slot],
                at_x(-offsets[slot]),
            ).wait_recv()
        is_low_q = low((q_half, LANES))
        for i in range(group):
            tile = jnp.concatenate([q_in[s, i] for s in range(side)], axis=0)
            zero = jnp.zeros_like(tile)
            qb[i, 0:q_half, :] = jnp.where(is_low_q, tile, zero)
            qb[i, q_half:q_all, :] = jnp.where(is_low_q, swap_halves(tile), zero)
        attend(
            [lambda i: text[i]],
            lambda shape: lax.broadcasted_iota(jnp.int32, shape, 1) < n_text,
            first=True,
        )

    def near():
        for slot in range(1, side):
            remote(
                pack_f.at[x],
                fresh.at[:, pl.ds(pl.multiple_of(wrap(x + offsets[slot]) * rows, rows), rows), :],
                xf_s.at[slot],
                xf_r.at[slot],
                at_x(-offsets[slot]),
            ).wait_recv()

        def keep(shape):
            row = lax.broadcasted_iota(jnp.int32, shape, 0)
            col = lax.broadcasted_iota(jnp.int32, shape, 1)
            patch = lax.shift_right_logical(
                jnp.bitwise_and(row, q_half - 1), half_rows.bit_length() - 1
            )
            slot = lax.shift_right_logical(col, rows.bit_length() - 1)
            far = lax.shift_right_logical(slot + 1, 1)
            source = x + jnp.where(jnp.bitwise_and(slot, 1) == 1, far, -far)
            source = jnp.where(source < 0, source + side, source)
            source = jnp.where(source >= side, source - side, source)
            stale_ok = jnp.logical_and(slot < side, source != patch)
            fresh_ok = slot - side == patch
            return jnp.logical_or(stale_ok, fresh_ok)

        attend([lambda i: kv[own, i], lambda i: fresh[i]], keep)

    def own_other():
        for u in range(SUBS):
            kv_shared(0, 0, u)
        attend([lambda i: kv[other(0, 0), i]])

    def piece_of(index, u, count):
        return lambda i: kv[index, i, u * sub : (u + count) * sub, :]

    def far(hops, u):
        def run():
            for direction in (0, 1):
                for v in (u, u + 1):
                    kv_shared(direction, hops, v)
            attend(
                [
                    piece_of(index(direction, hops), u, 2)
                    for index in (origin, other)
                    for direction in (0, 1)
                ]
            )

        return run

    def farthest():
        for u in range(SUBS):
            kv_shared(0, reach, u)
        attend([piece_of(origin(0, reach), 0, SUBS), piece_of(other(0, reach), 0, SUBS)])

    events = [(s, ((0, u), (1, u))) for s in range(1, reach) for u in range(SUBS)]
    events += [(reach, ((0, u), (1, u + SUBS // 2))) for u in range(SUBS // 2)]
    work = [(2, start_queries), (3, own_other)]
    for s in range(1, reach):
        for u in range(0, SUBS, 2):
            work.append(((s - 1) * SUBS + u + 2, far(s, u)))
    work.insert(5, (6, near))

    done = 0
    for number, (s, arrivals) in enumerate(events):
        for direction, u in arrivals:
            kv_arrival(direction, s, u)
            if s < reach and (s < reach - 1 or carries(direction, u)):
                go(kv_hop(direction, s, u))
            go(kv_share(direction, s, u))
        if done < len(work) and number >= work[done][0]:
            work[done][1]()
            done += 1
    for _, run in work[done:]:
        run()
    for direction in (0, 1):
        w_arrival(direction, 1)
        go(w_hop(direction, 1))
        go(w_share(direction, 1))
    farthest()

    is_low_o = low((q_half, LANES))
    for i in range(group):
        total = jnp.sum(l_s[i], axis=1, keepdims=True)
        attended = acc[i] / total
        top = pltpu.roll(attended[0:q_half], HEAD_DIM, 1)
        og[x, i] = jnp.where(is_low_o, top, attended[q_half:q_all]).astype(BF16)

    o_sub = q_half // O_SUBS

    def o_piece(direction, hops, u):
        return og.at[wrap(x - hops if direction == 0 else x + hops), :, pl.ds(u * o_sub, o_sub), :]

    def o_hop(direction, hops, u):
        piece = o_piece(direction, hops, u)
        return remote(
            piece,
            piece,
            xo_s.at[direction, hops, u],
            xo_r.at[direction, hops, u],
            at_x(1 if direction == 0 else -1),
        )

    def o_arrival(direction, hops, u):
        piece = o_piece(direction, hops, u)
        remote(
            piece,
            piece,
            xo_s.at[direction, hops - 1, u],
            xo_r.at[direction, hops - 1, u],
            at_x(-1 if direction == 0 else 1),
        ).wait_recv()

    def o_carries(direction, u):
        return (u < O_SUBS // 2) == (direction == 0)

    for u in range(O_SUBS):
        for direction in (0, 1):
            go(o_hop(direction, 0, u))
    early = [x_kv(o) for o in offsets[1:]] + [x_q(o) for o in offsets[1:]]
    early += [x_f(o) for o in offsets[1:]] + sends[: -2 * O_SUBS - 4]
    late = sends[-2 * O_SUBS - 4 :]
    sends = late
    for copy in early:
        copy.wait_send()

    for s in range(1, reach + 1):
        for u in range(O_SUBS):
            for direction in (0, 1):
                if s < reach or o_carries(direction, u):
                    o_arrival(direction, s, u)
                    if s < reach and (s < reach - 1 or o_carries(direction, u)):
                        go(o_hop(direction, s, u))
            if s == reach and u == 0:
                for index in range(2, side):
                    direction, hops = (0, index) if index <= reach else (1, index - reach)
                    if direction == 0:
                        w_shared(0, hops)
                    elif hops >= 2:
                        w_shared(1, hops)
                for index in range(0, 2 * side, 2):
                    pair = jnp.concatenate(
                        [wg[index].astype(F32), wg[index + 1].astype(F32)], axis=0
                    )
                    wcat[index * w_cols : (index + 2) * w_cols, :] = pair.astype(BF16)
        if s + 1 <= reach:
            for direction in (0, 1):
                if s + 1 < reach or direction == 0:
                    w_arrival(direction, s + 1)
                    if s + 1 < reach and (s + 1 < reach - 1 or direction == 0):
                        go(w_hop(direction, s + 1))
                    go(w_share(direction, s + 1))
        if s == 1:
            w_shared(0, 0)
            w_shared(0, 1)
            w_shared(1, 1)

    for pair in range(HEADS // 2):
        cols = slice(pair * LANES, (pair + 1) * LANES)
        even, odd = 2 * pair, 2 * pair + 1
        a, b = og[even // group, even % group], og[odd // group, odd % group]
        att[0:q_half, cols] = jnp.where(is_low_o, a, swap_halves(b))
        att[q_half:q_all, cols] = jnp.where(is_low_o, swap_halves(a), b)
    projected = lax.dot_general(
        att[...], wcat[...], (((1,), (1,)), ((), ())), preferred_element_type=F32
    )
    loads[8].wait()
    gating = gate_v[pl.ds(step_ref[0], 1), :]
    branch = (projected * gating).astype(BF16)
    for s in range(side):
        out_send[s, 0:half_rows, :] = branch[s * half_rows : (s + 1) * half_rows]
        out_send[s, half_rows:rows, :] = branch[
            q_half + s * half_rows : q_half + (s + 1) * half_rows
        ]

    def x_out(offset):
        return remote(
            out_send.at[wrap(x + offset)],
            out_in.at[x],
            oo_s.at[slot_of(offset)],
            oo_r.at[slot_of(-offset)],
            at_x(offset),
        )

    for o in offsets[1:]:
        go(x_out(o))
    out_in[x] = out_send[x]
    for copy in sends:
        copy.wait_send()
    for slot in range(1, side):
        remote(
            out_send.at[x],
            out_in.at[wrap(x + offsets[slot])],
            oo_s.at[slot],
            oo_r.at[slot],
            at_x(-offsets[slot]),
        ).wait_recv()
    for s in range(side):
        o_ref[:, s * block : (s + 1) * block] = out_in[s]


def solution(mesh):
    side = math.isqrt(mesh.shape["patch"] // 2)

    def body(q, fk, fv, sk, sv, tk, tv, w, gate, step):
        rows, width = q.shape
        group = HEADS // side
        chunk = side * rows
        q_half = chunk // 2
        depth, w_cols = w.shape
        block = w_cols * 2 * side
        n_text = tk.shape[0]
        text_rows = -(-n_text // LANES) * LANES
        reach = side // 2
        anywhere = pl.BlockSpec(memory_space=pl.ANY)
        dma = pltpu.SemaphoreType.DMA
        vmem = pltpu.VMEM
        return pl.pallas_call(
            functools.partial(kernel, side),
            out_shape=jax.ShapeDtypeStruct((rows, block * side), BF16),
            in_specs=[anywhere] * 9 + [pl.BlockSpec(memory_space=pltpu.SMEM)],
            out_specs=pl.BlockSpec(memory_space=pltpu.VMEM),
            scratch_shapes=[
                *[vmem((rows, width), BF16)] * 5,
                *[vmem((n_text, width), BF16)] * 2,
                vmem((depth, w_cols), BF16),
                vmem((gate.shape[0], block), F32),
                vmem((side, group, rows, LANES), BF16),
                vmem((side, group, rows // 2, LANES), BF16),
                vmem((side, group, rows, LANES), BF16),
                vmem((2 * side, group, chunk, LANES), BF16),
                vmem((group, chunk, LANES), BF16),
                vmem((side, group, rows // 2, LANES), BF16),
                vmem((group, 2 * q_half, LANES), BF16),
                vmem((group, text_rows, LANES), BF16),
                vmem((group, 2 * q_half, LANES), F32),
                vmem((group, 2 * q_half, LANES), F32),
                vmem((group, 2 * q_half, LANES), F32),
                vmem((side, group, q_half, LANES), BF16),
                vmem((2 * side, w_cols, depth), BF16),
                vmem((block, depth), BF16),
                vmem((2 * q_half, width), BF16),
                vmem((side, rows, block), BF16),
                vmem((side, rows, block), BF16),
                dma((9,)),
                *[dma((side,))] * 6,
                *[dma((2, reach, SUBS))] * 2,
                *[dma((side, SUBS))] * 2,
                *[dma((2, reach))] * 2,
                *[dma((side,))] * 2,
                *[dma((2, reach, O_SUBS))] * 2,
                *[dma((side,))] * 2,
            ],
            compiler_params=pltpu.CompilerParams(
                collective_id=0, has_side_effects=True, vmem_limit_bytes=48 * 1024 * 1024
            ),
        )(q, fk, fv, sk, sv, tk, tv, w, gate, step)

    rows_split = P(("groups", "patch"), None)
    in_specs = (rows_split,) * 5 + (P("groups", None),) * 2
    in_specs += (P(None, "patch"), P(), P("groups"))
    return jax.shard_map(body, mesh=mesh, in_specs=in_specs, out_specs=rows_split, check_vma=False)
```

time: 248 us -> 82 us (0.33)
  waiting for transfers between devices: 139 us -> 0 us
  Pallas kernels: 0 us -> 74.9 us
  local copies, waits for them, and re-layouts: 58.4 us -> 6.06 us
  matrix products: 25.8 us -> 0 us
  between operations: 14.2 us -> 0.74 us
  other arithmetic: 7.58 us -> 0 us
    all_gather x2 -> x0, waiting for transfers between devices: 138 us -> none  [the longest x1 128 us: sent_together(): lax.all_gather(both, axis, axis=dim, tiled=True)]
    pallas_call x0 -> x1, Pallas kernels: none -> 74.9 us  [body(): pl.pallas_call(functools.partial(kernel, side), out_shape=jax.ShapeDtypeS...]
    split x3 -> x0, local copies, waits for them, and re-layouts: 50.4 us -> none  [sent_together(): jnp.split(lax.all_gather(both, axis, axis=dim, tiled=True), ends, axis=al...]
    dot_general x6 -> x0, matrix products: 25.8 us -> none  [the longest x2 11.5 us: weigh(): jnp.einsum('ths,shd->thd', expo.astype(jnp.bfloat16), shaped, preferred_e...]
    concatenate x3 -> x0, other arithmetic: 4.15 us -> none  [the longest x1 1.7 us: sent_together(): both = jnp.concatenate(arrays, axis=along)]
    reduce_sum x2 -> x0, other arithmetic: 3.4 us -> none  [the longest x1 3 us: body(): new_sum = running_sum * shrink + jnp.sum(expo, -1)]
    unnamed x8 -> x18, local copies, waits for them, and re-layouts: 4.57 us -> 6.06 us
  transfers between devices with their start and end apart: 2 -> 0, of which waited for: 2 -> 0; matrix products, arithmetic and copies ran while one was open for 32% -> 0% of each run, Pallas kernels for 0% -> 0%
where the time goes in v1:
time: 82 us; the launch traced here: 81.7 us
  Pallas kernels  74.9 us (91%)
  local copies, waits for them, and re-layouts  6.06 us (7%)
    pallas_call x1, Pallas kernels, body(): pl.pallas_call(functools.partial(kernel, side), out_shape=jax.ShapeDtypeS...  74.9 us
    unnamed x18, local copies, waits for them, and re-layouts  6.06 us

profile of v1, /device:TPU:514, one launch (start us, length us, event | category | flops | bytes accessed | tf_op | source)
XLA Modules:
  0.0 81.7 jit_solution(16011900916129865066)
XLA Ops:
  0.7 0.0 copy-start.3
  0.7 0.0 copy-start.4
  0.7 0.0 copy-start.5
  0.7 0.0 copy-start.6
  0.7 1.2 %copy.11.w_hbm = bf16[1536,24]{1,0:T(8,128)(2,1)S(1)} copy(bf16[1536,24]{0,1:T(8,128)(2,1)} %param.17) | data formatting | bytes 147456 | tf_op args[7]
  1.9 0.0 copy-done.3
  1.9 0.0 copy-done.4
  1.9 0.0 copy-done.5
  1.9 0.0 copy-done.6
  1.9 0.0 copy-start
  1.9 1.1 %copy-done = bf16[226,1536]{1,0:T(8,128)(2,1)S(1)} copy-done((bf16[226,1536]{1,0:T(8,128)(2,1)S(1)}, bf16[226,1536]{1,0:T(8,128)(2,1)}, u32[]{:S(2)}) %copy-start) | copy-done | bytes 694296
  3.0 0.0 copy-start.1
  3.0 1.1 %copy-done.1 = bf16[226,1536]{1,0:T(8,128)(2,1)S(1)} copy-done((bf16[226,1536]{1,0:T(8,128)(2,1)S(1)}, bf16[226,1536]{1,0:T(8,128)(2,1)}, u32[]{:S(2)}) %copy-start.1) | copy-done | bytes 694296
  4.1 0.0 copy-start.2
  4.1 1.1 %copy-done.2 = f32[50,3072]{1,0:T(8,128)S(1)} copy-done((f32[50,3072]{1,0:T(8,128)S(1)}, f32[50,3072]{1,0:T(8,128)}, u32[]{:S(2)}) %copy-start.2) | copy-done | bytes 614424
  5.2 0.0 copy-start.7
  5.2 0.9 %copy-done.7 = bf16[32,1536]{1,0:T(8,128)(2,1)S(1)} copy-done((bf16[32,1536]{1,0:T(8,128)(2,1)S(1)}, bf16[32,1536]{1,0:T(8,128)(2,1)}, u32[]{:S(2)}) %copy-start.7) | copy-done | bytes 98328
  6.1 74.9 %shard_map.100 = bf16[32,3072]{1,0:T(8,128)(2,1)S(1)} custom-call(bf16[32,1536]{1,0:T(8,128)(2,1)S(1)} %copy-done.3, bf16[32,1536]{1,0:T(8,128)(2,1)S(1)} %copy-done.4, bf16[32,1536]{1,0:T(8,128)(2,1)S(1)} %copy-done.5, bf16[32,1536]{1,0:T(8,128)(2,1)S(1)} %copy-done.6, bf16[32,1536]{1,0:T(8,128)(2,1)S(1)} %copy-done.7, bf16[226,1536]{1,0:T(8,128)(2,1)S(1)} %copy-done, ...), custom_call_target="tpu_custom_call" | custom-call | tf_op jit(solution)/shard_map/pallas_call | solution.py:625
  81.0 0.7 copy.14
Async XLA Ops:
  0.7 1.2 %copy-start.3 = (bf16[32,1536]{1,0:T(8,128)(2,1)S(1)}, bf16[32,1536]{1,0:T(8,128)(2,1)}, u32[]{:S(2)}) copy-start(bf16[32,1536]{1,0:T(8,128)(2,1)} %q_hbm.1) | copy-start | bytes 294916
  0.7 1.2 %copy-start.4 = (bf16[32,1536]{1,0:T(8,128)(2,1)S(1)}, bf16[32,1536]{1,0:T(8,128)(2,1)}, u32[]{:S(2)}) copy-start(bf16[32,1536]{1,0:T(8,128)(2,1)} %fk_hbm.1) | copy-start | bytes 294916
  0.7 1.2 %copy-start.5 = (bf16[32,1536]{1,0:T(8,128)(2,1)S(1)}, bf16[32,1536]{1,0:T(8,128)(2,1)}, u32[]{:S(2)}) copy-start(bf16[32,1536]{1,0:T(8,128)(2,1)} %fv_hbm.1) | copy-start | bytes 294916
  0.7 1.2 %copy-start.6 = (bf16[32,1536]{1,0:T(8,128)(2,1)S(1)}, bf16[32,1536]{1,0:T(8,128)(2,1)}, u32[]{:S(2)}) copy-start(bf16[32,1536]{1,0:T(8,128)(2,1)} %sk_hbm.1) | copy-start | bytes 294916
  1.9 1.1 %copy-start = (bf16[226,1536]{1,0:T(8,128)(2,1)S(1)}, bf16[226,1536]{1,0:T(8,128)(2,1)}, u32[]{:S(2)}) copy-start(bf16[226,1536]{1,0:T(8,128)(2,1)} %tk_hbm.1) | copy-start | bytes 2082820
  3.0 1.1 %copy-start.1 = (bf16[226,1536]{1,0:T(8,128)(2,1)S(1)}, bf16[226,1536]{1,0:T(8,128)(2,1)}, u32[]{:S(2)}) copy-start(bf16[226,1536]{1,0:T(8,128)(2,1)} %tv_hbm.1) | copy-start | bytes 2082820
  4.1 1.1 %copy-start.2 = (f32[50,3072]{1,0:T(8,128)S(1)}, f32[50,3072]{1,0:T(8,128)}, u32[]{:S(2)}) copy-start(f32[50,3072]{1,0:T(8,128)} %gate_hbm.1) | copy-start | bytes 1843204
  5.2 0.9 %copy-start.7 = (bf16[32,1536]{1,0:T(8,128)(2,1)S(1)}, bf16[32,1536]{1,0:T(8,128)(2,1)}, u32[]{:S(2)}) copy-start(bf16[32,1536]{1,0:T(8,128)(2,1)} %sv_hbm.1) | copy-start | bytes 294916

commit v2 on v1

v2 whole, which is shorter than its diff:
```python
import functools
import math

import jax
import jax.numpy as jnp
from jax import lax
from jax.experimental import pallas as pl
from jax.experimental.pallas import tpu as pltpu
from jax.sharding import PartitionSpec as P

HEAD_DIM = 64
HEADS = 24
LANES = 128

OWN_FIRST = 6
LAG = 3
GROUPED = 4
O_SUBS = 4
MESH = pl.DeviceIdType.MESH
F32 = jnp.float32
BF16 = jnp.bfloat16


def swap_halves(tile):
    return pltpu.roll(tile.astype(F32), HEAD_DIM, 1).astype(tile.dtype)


def kernel(
    side,
    q_hbm,
    fk_hbm,
    fv_hbm,
    sk_hbm,
    sv_hbm,
    tk_hbm,
    tv_hbm,
    w_hbm,
    gate_hbm,
    step_ref,
    o_ref,
    q_v,
    fk_v,
    fv_v,
    sk_v,
    sv_v,
    tk_v,
    tv_v,
    gate_v,
    pack_kv,
    pack_q,
    pack_f,
    kv,
    fresh,
    q_in,
    qb,
    text,
    m_s,
    l_s,
    acc,
    og,
    wg,
    wcat,
    att,
    out_send,
    out_in,
    in_sem,
    xk_s,
    xk_r,
    xq_s,
    xq_r,
    xf_s,
    xf_r,
    yk_s,
    yk_r,
    ck_s,
    ck_r,
    yw_s,
    yw_r,
    cw_s,
    cw_r,
    xo_s,
    xo_r,
    oo_s,
    oo_r,
):
    rows = q_v.shape[0]
    half_rows = rows // 2
    group = HEADS // side
    q_half = side * half_rows
    q_all = 2 * q_half
    chunk = side * rows
    reach = side // 2
    subs = side
    n_text = tk_v.shape[0]
    w_cols = wg.shape[1]
    block = w_cols * 2 * side
    factor = HEAD_DIM ** (-0.5) * math.log2(math.e)

    me = lax.axis_index("patch")
    core = lax.rem(me, 2)
    y = lax.rem(lax.div(me, 2), side)
    x = lax.div(me, 2 * side)

    def wrap(value):
        return lax.rem(value + side, side)

    def at_x(offset):
        return {"patch": (wrap(x + offset) * side + y) * 2 + core}

    def at_y(offset):
        return {"patch": (x * side + wrap(y + offset)) * 2 + core}

    partner = {"patch": (x * side + y) * 2 + 1 - core}

    offsets = [0]
    for k in range(1, reach):
        offsets += [k, -k]
    offsets.append(reach)

    def slot_of(offset):
        return offsets.index(offset) if offset in offsets else offsets.index(offset + side)

    def remote(src, dst, send_sem, recv_sem, device):
        return pltpu.make_async_remote_copy(
            src_ref=src,
            dst_ref=dst,
            send_sem=send_sem,
            recv_sem=recv_sem,
            device_id=device,
            device_id_type=MESH,
        )

    own = y * 2 + core
    cols_x = pl.ds(pl.multiple_of(x * block, LANES), block)
    loads = [
        pltpu.make_async_copy(src, dst, in_sem.at[i])
        for i, (src, dst) in enumerate(
            [
                (sk_hbm, sk_v),
                (sv_hbm, sv_v),
                (q_hbm, q_v),
                (fk_hbm, fk_v),
                (fv_hbm, fv_v),
                (w_hbm, wg.at[own]),
                (tk_hbm, tk_v),
                (tv_hbm, tv_v),
                (gate_hbm.at[:, cols_x], gate_v),
            ]
        )
    ]
    for load in loads:
        load.start()

    barrier = pltpu.get_barrier_semaphore()
    peers = [at_x(o) for o in offsets[1:]] + [at_y(1), at_y(-1), partner]
    for peer in peers:
        pl.semaphore_signal(barrier, inc=1, device_id=peer, device_id_type=MESH)

    def settle(ref, sem):
        pltpu.make_async_copy(ref, ref, sem).wait()

    def low(shape):
        return lax.broadcasted_iota(jnp.int32, shape, 1) < HEAD_DIM

    def pack_pairs(k_ref, v_ref, out):
        is_low = low((rows, LANES))
        for pair in range(HEADS // 2):
            cols = slice(pair * LANES, (pair + 1) * LANES)
            k, v = k_ref[:, cols], v_ref[:, cols]
            even, odd = 2 * pair, 2 * pair + 1
            out[even // group, even % group] = jnp.where(is_low, k, swap_halves(v))
            out[odd // group, odd % group] = jnp.where(is_low, swap_halves(k), v)

    def origin(direction, hops):
        return wrap(y - hops if direction == 0 else y + hops) * 2 + core

    def kv_piece(index, u):
        return kv.at[index, u]

    def arrival_sem(direction, hops, u):
        if hops < reach - 1:
            return yk_r.at[hops * subs + u]
        return yk_r.at[hops * subs + u - (subs // 2 if direction else 0)]

    def kv_hop(direction, hops, u, source=None):
        piece = kv_piece(origin(direction, hops), u)
        return remote(
            source or piece,
            piece,
            yk_s,
            arrival_sem(direction, hops, u),
            at_y(1 if direction == 0 else -1),
        )

    def share_sem(hops, u):
        if hops == 0:
            return ck_r.at[0]
        half = u // GROUPED if hops < reach else (u % (subs // 2)) // (GROUPED // 2)
        return ck_r.at[1 + (hops - 1) * (subs // GROUPED) + half]

    def kv_share(direction, hops, u, source=None):
        piece = kv_piece(origin(direction, hops), u)
        return remote(source or piece, piece, ck_s, share_sem(hops, u), partner)

    def other(direction, hops):
        return wrap(y - hops if direction == 0 else y + hops) * 2 + 1 - core

    def carries(direction, u):
        return (u < subs // 2) == (direction == 0)

    def w_hop(direction, hops):
        piece = wg.at[origin(direction, hops)]
        return remote(piece, piece, yw_s, yw_r.at[hops], at_y(1 if direction == 0 else -1))

    def w_share(direction, hops):
        piece = wg.at[origin(direction, hops)]
        return remote(piece, piece, cw_s, cw_r, partner)

    def w_last():
        piece = wg.at[origin(0, reach - 2)]
        return remote(piece, piece, yw_s, yw_r.at[reach - 1], at_y(2))

    def w_forward(hops):
        settle(wg.at[0:2] if hops < reach else wg.at[0], yw_r.at[hops - 1])
        for direction in (0, 1):
            if hops < reach - 1:
                w_hop(direction, hops).start()
            if hops < reach or direction == 0:
                w_share(direction, hops).start()
        if hops == reach - 2:
            w_last().start()

    with jax.named_scope("load_kv"):
        loads[0].wait()
        loads[1].wait()
    with jax.named_scope("pack_kv"):
        pack_pairs(sk_v, sv_v, pack_kv)
    with jax.named_scope("barrier"):
        pl.semaphore_wait(barrier, len(peers))

    def x_kv(offset):
        back = slot_of(-offset)
        return remote(
            pack_kv.at[wrap(x + offset)],
            kv.at[own, back],
            xk_s,
            xk_r.at[back],
            at_x(offset),
        )

    def x_kv_wait(slot):
        settle(kv.at[own, slot], xk_r.at[slot])

    def own_piece(u):
        if u:
            with jax.named_scope(f"x_wait_{u}"):
                x_kv_wait(u)
        first = pack_kv.at[x] if u == 0 else None
        kv_hop(0, 0, u, first).start()
        kv_hop(1, 0, u, first).start()
        kv_share(0, 0, u, first).start()

    for o in [1, -1, reach, *offsets[3:-1]]:
        x_kv(o).start()
    own_piece(0)
    kv[own, 0] = pack_kv[x]

    loads[2].wait()
    is_low = low((half_rows, LANES))
    for pair in range(HEADS // 2):
        cols = slice(pair * LANES, (pair + 1) * LANES)
        top, bottom = q_v[0:half_rows, cols], q_v[half_rows:rows, cols]
        even, odd = 2 * pair, 2 * pair + 1
        pack_q[even // group, even % group] = jnp.where(is_low, top, swap_halves(bottom))
        pack_q[odd // group, odd % group] = jnp.where(is_low, swap_halves(top), bottom)

    def x_q(offset):
        return remote(
            pack_q.at[wrap(x + offset)],
            q_in.at[x],
            xq_s,
            xq_r,
            at_x(offset),
        )

    loads[3].wait()
    loads[4].wait()
    pack_pairs(fk_v, fv_v, pack_f)

    def x_f(offset):
        return remote(
            pack_f.at[wrap(x + offset)],
            fresh.at[x],
            xf_s,
            xf_r,
            at_x(offset),
        )

    for o in offsets[1:]:
        x_q(o).start()
    for o in offsets[1:]:
        x_f(o).start()
    q_in[x] = pack_q[x]
    fresh[x] = pack_f[x]


    loads[5].wait()
    w_hop(0, 0).start()
    w_hop(1, 0).start()
    w_share(0, 0).start()
    for u in range(1, OWN_FIRST):
        own_piece(u)

    loads[6].wait()
    loads[7].wait()
    text[:, text.shape[1] - 32 :, :] = jnp.zeros((group, 32, LANES), BF16)
    is_low_text = low((n_text, LANES))
    for i in range(group):
        head = x * group + i
        odd = jnp.broadcast_to(lax.rem(head, 2), (n_text, LANES)) == 1
        cols = pl.ds(pl.multiple_of(lax.div(head, 2) * LANES, LANES), LANES)
        k, v = tk_v[:, cols], tv_v[:, cols]
        k = jnp.where(odd, swap_halves(k), k)
        v = jnp.where(odd, v, swap_halves(v))
        text[i, 0:n_text, :] = jnp.where(is_low_text, k, v)

    def attend(pieces, keep=None, first=False):
        keys = [jnp.concatenate([p(i) for p in pieces], axis=0) for i in range(group)]
        scores = [
            lax.dot_general(qb[i], keys[i], (((1,), (1,)), ((), ())), preferred_element_type=F32)
            for i in range(group)
        ]
        if keep is not None:
            kept = keep(scores[0].shape)
            scores = [jnp.where(kept, score, -jnp.inf) for score in scores]
        width = scores[0].shape[1] // LANES
        for i in range(group):
            highest = jnp.max(scores[i], axis=1, keepdims=True)
            if first:
                new_m = jnp.broadcast_to(highest, (q_all, LANES))
            else:
                old_m = m_s[i]
                new_m = jnp.maximum(old_m, highest)
            expo = jnp.exp2((scores[i] - jnp.concatenate([new_m] * width, axis=1)) * factor)
            part = expo[:, 0:LANES]
            for k in range(1, width):
                part = part + expo[:, k * LANES : (k + 1) * LANES]
            weighted = jnp.dot(expo.astype(BF16), keys[i], preferred_element_type=F32)
            if first:
                l_s[i] = part
                acc[i] = weighted
            else:
                shrink = jnp.exp2((old_m - new_m) * factor)
                l_s[i] = l_s[i] * shrink + part
                acc[i] = acc[i] * shrink + weighted
            m_s[i] = new_m

    def start_queries():
        settle(q_in.at[1:side], xq_r)
        is_low_q = low((q_half, LANES))
        for i in range(group):
            tile = jnp.concatenate([q_in[s, i] for s in range(side)], axis=0)
            zero = jnp.zeros_like(tile)
            qb[i, 0:q_half, :] = jnp.where(is_low_q, tile, zero)
            qb[i, q_half:q_all, :] = jnp.where(is_low_q, swap_halves(tile), zero)
        attend(
            [lambda i: text[i]],
            lambda shape: lax.broadcasted_iota(jnp.int32, shape, 1) < n_text,
            first=True,
        )

    def stacked(tiles):
        return jnp.concatenate(tiles, axis=0)

    def piece_of(index, u, count):
        return lambda i: stacked([kv[index, v, i] for v in range(u, u + count)])

    def near():
        settle(pack_f.at[1:side], xf_r)

        def keep(shape):
            row = lax.broadcasted_iota(jnp.int32, shape, 0)
            col = lax.broadcasted_iota(jnp.int32, shape, 1)
            patch = lax.shift_right_logical(
                jnp.bitwise_and(row, q_half - 1), half_rows.bit_length() - 1
            )
            slot = lax.shift_right_logical(col, rows.bit_length() - 1)
            far = lax.shift_right_logical(slot + 1, 1)
            source = x + jnp.where(jnp.bitwise_and(slot, 1) == 1, far, -far)
            source = jnp.where(source < 0, source + side, source)
            source = jnp.where(source >= side, source - side, source)
            stale_ok = jnp.logical_and(slot < side, source != patch)
            fresh_ok = slot - side == patch
            return jnp.logical_or(stale_ok, fresh_ok)

        attend(
            [piece_of(own, 0, subs), lambda i: stacked([fresh[s, i] for s in range(side)])], keep
        )

    def own_other():
        settle(kv.at[0], ck_r.at[0])
        attend([piece_of(other(0, 0), 0, subs)])

    def far(hops, u):
        def run():
            settle(kv.at[0, 0 : 2 * GROUPED], share_sem(hops, u))
            attend(
                [
                    piece_of(index(direction, hops), u, GROUPED)
                    for index in (origin, other)
                    for direction in (0, 1)
                ]
            )

        return run

    def farthest(u):
        def run():
            settle(kv.at[0, 0:GROUPED], share_sem(reach, u))
            attend(
                [
                    piece_of(index(0, reach), v, GROUPED // 2)
                    for index in (origin, other)
                    for v in (u, u + subs // 2)
                ]
            )

        return run

    events = [(s, ((0, u), (1, u))) for s in range(1, reach) for u in range(subs)]
    events += [(reach, ((0, u), (1, u + subs // 2))) for u in range(subs // 2)]
    work = [(subs - 1, start_queries), (subs + LAG, own_other)]
    for s in range(1, reach):
        for u in range(0, subs, GROUPED):
            work.append(((s - 1) * subs + u + GROUPED - 1 + LAG, far(s, u)))
    work.append((2 * subs, near))
    work.append(((reach - 1) * subs + GROUPED // 2, farthest(0)))
    work = work[:1] + sorted(work[1:], key=lambda item: item[0])
    last = farthest(GROUPED // 2)
    late_own = {2 * k + 2: OWN_FIRST + k for k in range(subs - OWN_FIRST)}

    done = 0
    for number, (s, arrivals) in enumerate(events):
        if number in late_own:
            own_piece(late_own[number])
        if number == (reach - 1) * subs:
            w_forward(1)
        with jax.named_scope(f"ring_{s}_{arrivals[0][1]}"):
            settle(kv.at[0, 0:2], yk_r.at[number])
        for direction, u in arrivals:
            if s < reach and (s < reach - 1 or carries(direction, u)):
                kv_hop(direction, s, u).start()
            kv_share(direction, s, u).start()
        if done < len(work) and number >= work[done][0]:
            with jax.named_scope(f"work_{done}"):
                work[done][1]()
            done += 1
    for _, run in work[done:]:
        run()
    with jax.named_scope("farthest"):
        last()

    o_sub = q_half // O_SUBS
    is_low_o = low((q_half, LANES))
    for i in range(group):
        total = jnp.sum(l_s[i], axis=1, keepdims=True)
        attended = acc[i] / total
        top = pltpu.roll(attended[0:q_half], HEAD_DIM, 1)
        both = jnp.where(is_low_o, top, attended[q_half:q_all]).astype(BF16)
        for u in range(O_SUBS):
            og[x, u, i] = both[u * o_sub : (u + 1) * o_sub]

    def o_piece(direction, hops, u):
        return og.at[wrap(x - hops if direction == 0 else x + hops), u]

    def o_hop(direction, hops, u):
        piece = o_piece(direction, hops, u)
        return remote(
            piece, piece, xo_s, xo_r.at[hops * O_SUBS + u], at_x(1 if direction == 0 else -1)
        )

    def o_last(direction, u):
        piece = o_piece(direction, reach - 2, u)
        sem = xo_r.at[(reach - 1) * O_SUBS + u]
        return remote(piece, piece, xo_s, sem, at_x(2 if direction == 0 else -2))

    def o_carries(direction, u):
        return (u < O_SUBS // 2) == (direction == 0)

    for u in range(O_SUBS):
        for direction in (0, 1):
            o_hop(direction, 0, u).start()
    w_forward(2)
    settle(pack_kv.at[1:side], xk_s)
    settle(pack_q.at[1:side], xq_s)
    settle(pack_f.at[1:side], xf_s)
    settle(kv.at[1:side], yk_s)
    settle(kv.at[0:side], ck_s)

    for s in range(1, reach + 1):
        for u in range(O_SUBS):
            with jax.named_scope(f"o_{s}_{u}"):
                settle(og.at[0, 0 : 1 if s == reach else 2], xo_r.at[(s - 1) * O_SUBS + u])
            for direction in (0, 1):
                if s < reach - 1:
                    o_hop(direction, s, u).start()
                if s == reach - 2 and o_carries(direction, u):
                    o_last(direction, u).start()
        with jax.named_scope(f"w_{s}"):
            if s < reach - 2:
                w_forward(s + 2)
            if s == reach - 2:
                w_forward(reach)
        if s == reach - 1:
            with jax.named_scope("w_all"):
                settle(wg.at[0:side], cw_r)
                settle(wg.at[1:side], yw_s)
                settle(wg.at[0:side], cw_s)
                for index in range(0, 2 * side, 2):
                    pair = jnp.concatenate(
                        [wg[index].astype(F32), wg[index + 1].astype(F32)], axis=0
                    )
                    wcat[index * w_cols : (index + 2) * w_cols, :] = pair.astype(BF16)

    for pair in range(HEADS // 2):
        cols = slice(pair * LANES, (pair + 1) * LANES)
        even, odd = 2 * pair, 2 * pair + 1
        a, b = (
            stacked([og[h // group, u, h % group] for u in range(O_SUBS)]) for h in (even, odd)
        )
        att[0:q_half, cols] = jnp.where(is_low_o, a, swap_halves(b))
        att[q_half:q_all, cols] = jnp.where(is_low_o, swap_halves(a), b)
    projected = lax.dot_general(
        att[...], wcat[...], (((1,), (1,)), ((), ())), preferred_element_type=F32
    )
    loads[8].wait()
    gating = gate_v[pl.ds(step_ref[0], 1), :]
    branch = (projected * gating).astype(BF16)
    for s in range(side):
        out_send[s, 0:half_rows, :] = branch[s * half_rows : (s + 1) * half_rows]
        out_send[s, half_rows:rows, :] = branch[
            q_half + s * half_rows : q_half + (s + 1) * half_rows
        ]

    def x_out(offset):
        return remote(
            out_send.at[wrap(x + offset)],
            out_in.at[x],
            oo_s,
            oo_r,
            at_x(offset),
        )

    for o in offsets[:0:-1]:
        x_out(o).start()
    out_in[x] = out_send[x]
    with jax.named_scope("late"):
        settle(og.at[1:side], xo_s)
        settle(out_send.at[1:side], oo_s)
    with jax.named_scope("out_wait"):
        settle(out_in.at[1:side], oo_r)
    for s in range(side):
        o_ref[:, s * block : (s + 1) * block] = out_in[s]


def solution(mesh):
    side = math.isqrt(mesh.shape["patch"] // 2)

    def body(q, fk, fv, sk, sv, tk, tv, w, gate, step):
        w = w.T
        rows, width = q.shape
        group = HEADS // side
        chunk = side * rows
        q_half = chunk // 2
        w_cols, depth = w.shape
        block = w_cols * 2 * side
        n_text = tk.shape[0]
        text_rows = -(-n_text // LANES) * LANES
        reach, subs = side // 2, side
        anywhere = pl.BlockSpec(memory_space=pltpu.HBM)
        dma = pltpu.SemaphoreType.DMA
        vmem = pltpu.VMEM
        return pl.pallas_call(
            functools.partial(kernel, side),
            out_shape=jax.ShapeDtypeStruct((rows, block * side), BF16),
            in_specs=[anywhere] * 9 + [pl.BlockSpec(memory_space=pltpu.SMEM)],
            out_specs=pl.BlockSpec(memory_space=pltpu.VMEM),
            scratch_shapes=[
                *[vmem((rows, width), BF16)] * 5,
                *[vmem((n_text, width), BF16)] * 2,
                vmem((gate.shape[0], block), F32),
                vmem((side, group, rows, LANES), BF16),
                vmem((side, group, rows // 2, LANES), BF16),
                vmem((side, group, rows, LANES), BF16),
                vmem((2 * side, side, group, rows, LANES), BF16),
                vmem((side, group, rows, LANES), BF16),
                vmem((side, group, rows // 2, LANES), BF16),
                vmem((group, 2 * q_half, LANES), BF16),
                vmem((group, text_rows, LANES), BF16),
                vmem((group, 2 * q_half, LANES), F32),
                vmem((group, 2 * q_half, LANES), F32),
                vmem((group, 2 * q_half, LANES), F32),
                vmem((side, O_SUBS, group, q_half // O_SUBS, LANES), BF16),
                vmem((2 * side, w_cols, depth), BF16),
                vmem((block, depth), BF16),
                vmem((2 * q_half, width), BF16),
                vmem((side, rows, block), BF16),
                vmem((side, rows, block), BF16),
                dma((9,)),
                dma,
                dma((side,)),
                *[dma] * 5,
                dma(((reach - 1) * subs + subs // 2,)),
                dma,
                dma((1 + (reach - 1) * (subs // GROUPED) + 2,)),
                dma,
                dma((reach,)),
                dma,
                dma,
                dma,
                dma((reach * O_SUBS,)),
                dma,
                dma,
            ],
            compiler_params=pltpu.CompilerParams(
                collective_id=0, has_side_effects=True, vmem_limit_bytes=48 * 1024 * 1024
            ),
        )(
            *(
                pltpu.with_memory_space_constraint(a, pltpu.HBM)
                for a in (q, fk, fv, sk, sv, tk, tv, w, gate)
            ),
            step,
        )

    rows_split = P(("groups", "patch"), None)
    in_specs = (rows_split,) * 5 + (P("groups", None),) * 2
    in_specs += (P(None, "patch"), P(), P("groups"))
    return jax.shard_map(body, mesh=mesh, in_specs=in_specs, out_specs=rows_split, check_vma=False)
```

time: 82 us -> 69.5 us (0.85); the launches traced: 81.7 us -> 68.1 us
  Pallas kernels: 74.9 us -> 66.8 us
  local copies, waits for them, and re-layouts: 6.06 us -> 0.68 us
    pallas_call x1, Pallas kernels: 74.9 us -> 66.8 us  [body(): pl.pallas_call(functools.partial(kernel, side), out_shape=jax.ShapeDtypeS...]
    unnamed x18 -> x1, local copies, waits for them, and re-layouts: 6.06 us -> 0.68 us
where the time goes in v2:
time: 69.5 us; the launch traced here: 68.1 us
  Pallas kernels  66.8 us (96%)
    pallas_call x1, Pallas kernels, body(): pl.pallas_call(functools.partial(kernel, side), out_shape=jax.ShapeDtypeS...  66.8 us

profile of v2, /device:TPU:514, one launch (start us, length us, event | category | flops | bytes accessed | tf_op | source)
XLA Modules:
  0.0 68.1 jit_solution(10069795803061179183)
XLA Ops:
  0.7 66.8 %shard_map.100 = bf16[32,3072]{1,0:T(8,128)(2,1)S(1)} custom-call(bf16[32,1536]{1,0:T(8,128)(2,1)} %q_hbm.1, bf16[32,1536]{1,0:T(8,128)(2,1)} %fk_hbm.1, bf16[32,1536]{1,0:T(8,128)(2,1)} %fv_hbm.1, bf16[32,1536]{1,0:T(8,128)(2,1)} %sk_hbm.1, bf16[32,1536]{1,0:T(8,128)(2,1)} %sv_hbm.1, bf16[226,1536]{1,0:T(8,128)(2,1)} %tk_hbm.1, bf16[226,1536]{1,0:T(8,128)(2,1)} %tv_hbm.1, ...), custom_call_target="tpu_custom_call" | custom-call | tf_op jit(solution)/shard_map/pallas_call | solution.py:583
  67.4 0.7 copy.13

commit v3 on v2

--- a/solution.py
+++ b/solution.py
@@ -62,7 +62,6 @@
     wcat,
     att,
     out_send,
-    out_in,
     in_sem,
     xk_s,
     xk_r,
@@ -148,13 +147,15 @@
             ]
         )
     ]
-    for load in loads:
+    for load in loads[:2]:
         load.start()
 
     barrier = pltpu.get_barrier_semaphore()
-    peers = [at_x(o) for o in offsets[1:]] + [at_y(1), at_y(-1), partner]
+    peers = [at_x(o) for o in offsets[:0:-1]] + [at_y(1), at_y(-1), partner]
     for peer in peers:
         pl.semaphore_signal(barrier, inc=1, device_id=peer, device_id_type=MESH)
+    for load in loads[2:]:
+        load.start()
 
     def settle(ref, sem):
         pltpu.make_async_copy(ref, ref, sem).wait()
@@ -208,27 +209,37 @@
     def carries(direction, u):
         return (u < subs // 2) == (direction == 0)
 
-    def w_hop(direction, hops):
-        piece = wg.at[origin(direction, hops)]
-        return remote(piece, piece, yw_s, yw_r.at[hops], at_y(1 if direction == 0 else -1))
+    def w_copy(direction, hops, links, lanes):
+        piece = wg.at[origin(direction, hops), :, lanes]
+        sem = yw_r.at[min(hops, 1)]
+        return remote(piece, piece, yw_s, sem, at_y(links if direction == 0 else -links))
 
     def w_share(direction, hops):
         piece = wg.at[origin(direction, hops)]
         return remote(piece, piece, cw_s, cw_r, partner)
 
-    def w_last():
-        piece = wg.at[origin(0, reach - 2)]
-        return remote(piece, piece, yw_s, yw_r.at[reach - 1], at_y(2))
-
-    def w_forward(hops):
-        settle(wg.at[0:2] if hops < reach else wg.at[0], yw_r.at[hops - 1])
+    width = wg.shape[2]
+    w_halves = (pl.ds(0, width // 2), pl.ds(width // 2, width // 2))
+
+    def w_first():
         for direction in (0, 1):
-            if hops < reach - 1:
-                w_hop(direction, hops).start()
-            if hops < reach or direction == 0:
+            w_copy(direction, 0, 1, pl.ds(0, width)).start()
+        w_share(0, 0).start()
+
+    def w_second():
+        settle(wg.at[0:2], yw_r.at[0])
+        for direction in (0, 1):
+            w_copy(direction, 1, reach - 1, w_halves[direction]).start()
+            for links in range(reach - 2, 0, -1):
+                w_copy(direction, 1, links, pl.ds(0, width)).start()
+            w_share(direction, 1).start()
+
+    def w_third():
+        settle(wg.at[0 : side - 3], yw_r.at[1])
+        for hops in range(2, reach):
+            for direction in (0, 1):
                 w_share(direction, hops).start()
-        if hops == reach - 2:
-            w_last().start()
+        w_share(0, reach).start()
 
     with jax.named_scope("load_kv"):
         loads[0].wait()
@@ -260,7 +271,7 @@
         kv_hop(1, 0, u, first).start()
         kv_share(0, 0, u, first).start()
 
-    for o in [1, -1, reach, *offsets[3:-1]]:
+    for o in offsets[1:]:
         x_kv(o).start()
     own_piece(0)
     kv[own, 0] = pack_kv[x]
@@ -304,10 +315,6 @@
     fresh[x] = pack_f[x]
 
 
-    loads[5].wait()
-    w_hop(0, 0).start()
-    w_hop(1, 0).start()
-    w_share(0, 0).start()
     for u in range(1, OWN_FIRST):
         own_piece(u)
 
@@ -444,7 +451,8 @@
         if number in late_own:
             own_piece(late_own[number])
         if number == (reach - 1) * subs:
-            w_forward(1)
+            loads[5].wait()
+            w_first()
         with jax.named_scope(f"ring_{s}_{arrivals[0][1]}"):
             settle(kv.at[0, 0:2], yk_r.at[number])
         for direction, u in arrivals:
@@ -464,9 +472,10 @@
     is_low_o = low((q_half, LANES))
     for i in range(group):
         total = jnp.sum(l_s[i], axis=1, keepdims=True)
-        attended = acc[i] / total
-        top = pltpu.roll(attended[0:q_half], HEAD_DIM, 1)
-        both = jnp.where(is_low_o, top, attended[q_half:q_all]).astype(BF16)
+        weighted = jnp.where(
+            is_low_o, pltpu.roll(acc[i, 0:q_half], HEAD_DIM, 1), acc[i, q_half:q_all]
+        )
+        both = (weighted / jnp.where(is_low_o, total[0:q_half], total[q_half:q_all])).astype(BF16)
         for u in range(O_SUBS):
             og[x, u, i] = both[u * o_sub : (u + 1) * o_sub]
 
@@ -479,18 +488,13 @@
             piece, piece, xo_s, xo_r.at[hops * O_SUBS + u], at_x(1 if direction == 0 else -1)
         )
 
-    def o_last(direction, u):
-        piece = o_piece(direction, reach - 2, u)
-        sem = xo_r.at[(reach - 1) * O_SUBS + u]
-        return remote(piece, piece, xo_s, sem, at_x(2 if direction == 0 else -2))
-
     def o_carries(direction, u):
         return (u < O_SUBS // 2) == (direction == 0)
 
     for u in range(O_SUBS):
         for direction in (0, 1):
             o_hop(direction, 0, u).start()
-    w_forward(2)
+    w_second()
     settle(pack_kv.at[1:side], xk_s)
     settle(pack_q.at[1:side], xq_s)
     settle(pack_f.at[1:side], xf_s)
@@ -502,16 +506,11 @@
             with jax.named_scope(f"o_{s}_{u}"):
                 settle(og.at[0, 0 : 1 if s == reach else 2], xo_r.at[(s - 1) * O_SUBS + u])
             for direction in (0, 1):
-                if s < reach - 1:
+                if s < reach and (s < reach - 1 or o_carries(direction, u)):
                     o_hop(direction, s, u).start()
-                if s == reach - 2 and o_carries(direction, u):
-                    o_last(direction, u).start()
-        with jax.named_scope(f"w_{s}"):
-            if s < reach - 2:
-                w_forward(s + 2)
-            if s == reach - 2:
-                w_forward(reach)
         if s == reach - 1:
+            with jax.named_scope("w_third"):
+                w_third()
             with jax.named_scope("w_all"):
                 settle(wg.at[0:side], cw_r)
                 settle(wg.at[1:side], yw_s)
@@ -522,6 +521,14 @@
                     )
                     wcat[index * w_cols : (index + 2) * w_cols, :] = pair.astype(BF16)
 
+    loads[8].wait()
+    gating = gate_v[pl.ds(step_ref[0], 1), :]
+
+    def x_out(offset):
+        return remote(
+            out_send.at[wrap(x + offset)], o_ref.at[:, cols_x], oo_s, oo_r, at_x(offset)
+        )
+
     for pair in range(HEADS // 2):
         cols = slice(pair * LANES, (pair + 1) * LANES)
         even, odd = 2 * pair, 2 * pair + 1
@@ -533,34 +540,21 @@
     projected = lax.dot_general(
         att[...], wcat[...], (((1,), (1,)), ((), ())), preferred_element_type=F32
     )
-    loads[8].wait()
-    gating = gate_v[pl.ds(step_ref[0], 1), :]
     branch = (projected * gating).astype(BF16)
     for s in range(side):
-        out_send[s, 0:half_rows, :] = branch[s * half_rows : (s + 1) * half_rows]
-        out_send[s, half_rows:rows, :] = branch[
-            q_half + s * half_rows : q_half + (s + 1) * half_rows
-        ]
-
-    def x_out(offset):
-        return remote(
-            out_send.at[wrap(x + offset)],
-            out_in.at[x],
-            oo_s,
-            oo_r,
-            at_x(offset),
-        )
-
+        for part in range(2):
+            start = part * q_half + s * half_rows
+            out_send[s, part * half_rows : (part + 1) * half_rows] = branch[
+                start : start + half_rows
+            ]
     for o in offsets[:0:-1]:
         x_out(o).start()
-    out_in[x] = out_send[x]
+    o_ref[:, cols_x] = out_send[x]
     with jax.named_scope("late"):
         settle(og.at[1:side], xo_s)
         settle(out_send.at[1:side], oo_s)
     with jax.named_scope("out_wait"):
-        settle(out_in.at[1:side], oo_r)
-    for s in range(side):
-        o_ref[:, s * block : (s + 1) * block] = out_in[s]
+        settle(out_send.at[1:side], oo_r)
 
 
 def solution(mesh):
@@ -605,7 +599,6 @@
                 vmem((block, depth), BF16),
                 vmem((2 * q_half, width), BF16),
                 vmem((side, rows, block), BF16),
-                vmem((side, rows, block), BF16),
                 dma((9,)),
                 dma,
                 dma((side,)),

time: 69.5 us -> 68.3 us (0.983); the launches traced: 68.1 us -> 68.2 us
  no operation moved by 1% of the time
where the time goes in v3:
time: 68.3 us; the launch traced here: 68.2 us
  Pallas kernels  66.9 us (98%)
    pallas_call x1, Pallas kernels, body(): pl.pallas_call(functools.partial(kernel, side), out_shape=jax.ShapeDtypeS...  66.9 us

profile of v3, /device:TPU:514, one launch (start us, length us, event | category | flops | bytes accessed | tf_op | source)
XLA Modules:
  0.0 68.2 jit_solution(9316350063112747182)
XLA Ops:
  0.7 66.9 %shard_map.100 = bf16[32,3072]{1,0:T(8,128)(2,1)S(1)} custom-call(bf16[32,1536]{1,0:T(8,128)(2,1)} %q_hbm.1, bf16[32,1536]{1,0:T(8,128)(2,1)} %fk_hbm.1, bf16[32,1536]{1,0:T(8,128)(2,1)} %fv_hbm.1, bf16[32,1536]{1,0:T(8,128)(2,1)} %sk_hbm.1, bf16[32,1536]{1,0:T(8,128)(2,1)} %sv_hbm.1, bf16[226,1536]{1,0:T(8,128)(2,1)} %tk_hbm.1, bf16[226,1536]{1,0:T(8,128)(2,1)} %tv_hbm.1, ...), custom_call_target="tpu_custom_call" | custom-call | tf_op jit(solution)/shard_map/pallas_call | solution.py:577
  67.5 0.7 copy.13
